TPU v7x, 32 devices: a whole 2x2x4 slice. The times are simulated.
32 devices in a mesh: gx: 4 (over z), gy: 4 (over y, x), gz: 2 (over core).
Axes of the slice: x: 2, y: 2, z: 4, core: 2. Of those that a mesh axis runs over, the one named last changes fastest.
Arguments:
- panel: float32 [8192, 4096], P(('gx', 'gy', 'gz'))
- treat_start: int32 [8192], P(('gx', 'gy', 'gz')), may hold values from 1024 to 4096
- loading_init: float32 [64, 8192], P(None, ('gx', 'gy', 'gz'))
- factor_init: float32 [64, 4096], P(None, ('gx', 'gy', 'gz'))
- unit_init: float32 [8192], P(('gx', 'gy', 'gz'))
- day_init: float32 [4096], replicated
Outputs:
- loading_out: float32 [64, 8192], P(None, ('gx', 'gy', 'gz'))
- factor_out: float32 [64, 4096], P(None, ('gx', 'gy', 'gz'))
- unit_out: float32 [8192], P(('gx', 'gy', 'gz'))
- day_out: float32 [4096], replicated
Inputs may be any that keep to these rules, and one draw needn't show every extreme that they name: A unit is treated from day treat_start on; 4096 means never treated.
All inputs are finite; a program needn't handle non-finite values.
Results may differ from a plain program's by a relative error of at most 0.0001.
Values sent between devices are 32-bit elements; how exact they have to be, the bound alone decides.
A program may use at most 64 MiB of HBM per device.

v0:
```python
import jax
import jax.numpy as jnp
from jax import lax
from jax.sharding import PartitionSpec as P

SWEEPS = 2
RIDGE = 1.0


def solve_spd(matrix, right):
    lower = jnp.linalg.cholesky(matrix)
    middle = lax.linalg.triangular_solve(lower, right, left_side=True, lower=True)
    return lax.linalg.triangular_solve(lower, middle, left_side=True, lower=True, transpose_a=True)


def contract_first(left, right):
    return lax.dot_general(
        left,
        right,
        (((0,), (0,)), ((), ())),
        precision=lax.Precision.HIGHEST,
        preferred_element_type=jnp.float32,
    )


def contract_last(left, right):
    return lax.dot_general(
        left,
        right,
        (((1,), (1,)), ((), ())),
        precision=lax.Precision.HIGHEST,
        preferred_element_type=jnp.float32,
    )


def body(panel, treat_start, loading_init, factor_init, unit_init, day_init):
    unit_rows, total_days = panel.shape
    devices = lax.axis_size(("gx", "gy", "gz"))
    all_units = unit_rows * devices
    slice_days = factor_init.shape[1]
    rank = loading_init.shape[0]
    ridge_eye = jnp.eye(rank, dtype=jnp.float32) * RIDGE
    observed = lax.broadcasted_iota(jnp.int32, (unit_rows, total_days), 1) < treat_start[:, None]
    loading = loading_init
    unit_eff = unit_init
    day_eff = day_init
    factors = None
    owned_factors = factor_init
    for sweep_index in range(SWEEPS):
        unit_gram = lax.psum(contract_last(loading, loading), ("gx", "gy", "gz"))
        if sweep_index == 0:
            fitted = contract_first(
                loading, lax.all_gather(factor_init, ("gx", "gy", "gz"), axis=1, tiled=True)
            )
        else:
            fitted = contract_first(loading, factors)
        imputed = jnp.where(observed, panel, unit_eff[:, None] + day_eff[None, :] + fitted)
        without = imputed - fitted
        day_part = jnp.sum(without, 0)
        row_sums = jnp.sum(without, 1)
        resid = None
        day_sums = lax.psum(day_part, ("gx", "gy", "gz"))
        grand = jnp.sum(day_sums) / (all_units * total_days)
        day_eff = day_sums / all_units - grand
        unit_eff = row_sums / total_days - grand
        resid = imputed - unit_eff[:, None] - day_eff[None, :]
        payload = jnp.dot(loading, resid, precision=lax.Precision.HIGHEST)
        summed = lax.psum(payload, ("gx", "gy", "gz"))
        factors = solve_spd(unit_gram + ridge_eye, summed)
        owned_factors = lax.dynamic_slice_in_dim(
            factors, lax.axis_index(("gx", "gy", "gz")) * slice_days, slice_days, 1
        )
        factor_gram = jnp.dot(factors, factors.T, precision=lax.Precision.HIGHEST)
        loading = solve_spd(factor_gram + ridge_eye, contract_last(factors, resid))
    return (loading, owned_factors, unit_eff, day_eff)


def solution(mesh):
    return jax.shard_map(
        body,
        mesh=mesh,
        in_specs=(
            P(("gx", "gy", "gz"), None),
            P(("gx", "gy", "gz")),
            P(None, ("gx", "gy", "gz")),
            P(None, ("gx", "gy", "gz")),
            P(("gx", "gy", "gz")),
            P(),
        ),
        out_specs=(
            P(None, ("gx", "gy", "gz")),
            P(None, ("gx", "gy", "gz")),
            P(("gx", "gy", "gz")),
            P(),
        ),
        check_vma=False,
    )
```

profile of v0, /device:TPU:0, one launch (start us, length us, event | category | flops | bytes accessed | tf_op | source)
XLA Modules:
  0.0 507.0 jit_solution(17631101533937465551)
XLA Ops:
  8.3 57.7 %all-gather.2.cloned.1.call-done = f32[64,4096]{1,0:T(8,128)} async-done(((f32[64,128]{1,0:T(8,128)}), f32[64,4096]{1,0:T(8,128)}) %all-gather.2.cloned.1.call-update) | async-done | bytes 1048592 | tf_op jit(solution)/shard_map/all_gather | solution.py:53
  65.9 7.9 %subtract_reduce_fusion.3 = (f32[256]{0:T(256)S(1)}, f32[4096]{0:T(1024)S(1)}, f32[256,4096]{1,0:T(8,128)}) fusion(f32[256,4096]{1,0:T(8,128)} %param.15, f32[4096]{0:T(1024)} %param.20, f32[256]{0:T(256)} %param.19, s32[256]{0:T(256)} %param.16, f32[64,256]{1,0:T(8,128)S(1)} %copy-done, f32[64,4096]{1,0:T(8,128)} %all-gather.2.cloned.1.call-done), kind=kOutput, calls=%fused_computation.20 | convolution fusion | flops 812642048 | bytes 9538560 | tf_op jit(solution)/shard_map/dot_general | solution.py:17
  73.8 40.5 %all-reduce.1 = (f32[4096]{0:T(1024)S(1)}, f32[64,64]{0,1:T(8,128)S(1)}) all-reduce(f32[4096]{0:T(1024)S(1)} %get-tuple-element.12, f32[64,64]{0,1:T(8,128)S(1)} %fusion.41), channel_id=1, replica_groups=mesh['gx'=4,'gy'=4,'gz'=2] {'gx','gy','gz'}, use_global_device_ids=true, to_apply=%region_5.0 | all-reduce | flops 8192 | bytes 65536 | tf_op jit(solution)/shard_map/psum | solution.py:62
  115.6 12.0 %convolution_bitcast_fusion = f32[64,4096]{0,1:T(8,128)} fusion(f32[64,256]{1,0:T(8,128)S(1)} %copy-done, f32[4096]{0:T(1024)S(1)} %multiply_subtract_fusion.1, f32[256]{0:T(256)S(1)} %multiply_subtract_fusion.3, f32[256,4096]{1,0:T(8,128)} %param.15, f32[256,4096]{1,0:T(8,128)} %get-tuple-element.17, f32[4096]{0:T(1024)S(1)} %copy-done.3, ...), kind=kOutput, calls=%fused_computation | convolution fusion | flops 811597824 | bytes 9538560 | tf_op jit(solution)/shard_map/dot_general | solution.py:67
  127.6 10.1 %all-reduce.7.cloned.1.call-start = ((), (), s32[]{:S(2)}) async-start(), calls=%async_computation.2 | async-start | bytes 2097152 | tf_op jit(solution)/shard_map/psum | solution.py:68
  137.8 5.8 %cholesky.74 = f32[64,64]{1,0:T(8,128)S(1)} custom-call(f32[64,64]{1,0:T(8,128)S(1)} %fusion.34), custom_call_target="Cholesky" | custom-call | tf_op jit(solution)/shard_map/jit(cholesky)/cholesky | solution.py:11
  145.0 4.9 custom-call.19
  149.9 111.7 %all-reduce.5.cloned.1.call-done = f32[64,4096]{0,1:T(8,128)} async-done(((f32[64,4096]{0,1:T(8,128)}), f32[64,4096]{0,1:T(8,128)}) %all-reduce.5.cloned.1.call-update) | async-done | bytes 1048592 | tf_op jit(solution)/shard_map/psum | solution.py:68
  261.6 4.1 fusion.30
  265.7 1.0 fusion.32
  267.7 6.6 %fusion = f32[64,256]{1,0:T(8,128)S(1)} fusion(f32[64,4096]{1,0:T(8,128)S(1)} %fusion.32, f32[4096]{0:T(1024)S(1)} %multiply_subtract_fusion.1, f32[256]{0:T(256)S(1)} %multiply_subtract_fusion.3, f32[256,4096]{1,0:T(8,128)S(1)} %copy-done.1, f32[256,4096]{1,0:T(8,128)} %get-tuple-element.17, f32[4096]{0:T(1024)S(1)} %copy-done.3, f32[256]{0:T(256)S(1)} %copy-done.6, ...), kind=kOutput, calls=%fused_computation.6 | convolution fusion | flops 811597824 | bytes 9538560 | tf_op jit(solution)/shard_map/dot_general | solution.py:27
  274.4 5.8 %cholesky.85 = f32[64,64]{1,0:T(8,128)S(1)} custom-call(f32[64,64]{1,0:T(8,128)S(1)} %fusion.29), custom_call_target="Cholesky" | custom-call | tf_op jit(solution)/shard_map/jit(cholesky)/cholesky | solution.py:11
  281.6 4.9 custom-call.21
  287.0 7.7 %subtract_reduce_fusion.1 = (f32[256]{0:T(256)S(1)}, f32[4096]{0:T(1024)S(1)}, f32[256,4096]{1,0:T(8,128)}) fusion(f32[256,4096]{1,0:T(8,128)} %param.15, f32[4096]{0:T(1024)S(1)} %multiply_subtract_fusion.1, f32[256]{0:T(256)S(1)} %multiply_subtract_fusion.3, s32[256]{0:T(256)S(1)} %copy-done.5, f32[64,256]{1,0:T(8,128)S(1)} %fusion.27, ...), kind=kOutput, calls=%fused_computation.18 | convolution fusion | flops 812642048 | bytes 9538560 | tf_op jit(solution)/shard_map/dot_general | solution.py:17
  294.9 39.5 %all-reduce = (f32[4096]{0:T(1024)S(1)}, f32[64,64]{0,1:T(8,128)S(1)}) all-reduce(f32[4096]{0:T(1024)S(1)} %get-tuple-element.10, f32[64,64]{0,1:T(8,128)S(1)} %fusion.42), channel_id=1, replica_groups=mesh['gx'=4,'gy'=4,'gz'=2] {'gx','gy','gz'}, use_global_device_ids=true, to_apply=%region_11.17 | all-reduce | flops 8192 | bytes 65536 | tf_op jit(solution)/shard_map/psum | solution.py:62
  335.9 8.1 %fusion.2 = f32[64,4096]{1,0:T(8,128)} fusion(f32[64,256]{1,0:T(8,128)S(1)} %fusion.27, f32[4096]{0:T(1024)S(1)} %multiply_subtract_fusion, f32[256]{0:T(256)S(1)} %multiply_subtract_fusion.2, f32[256,4096]{1,0:T(8,128)} %param.15, f32[256,4096]{1,0:T(8,128)} %get-tuple-element.18, f32[4096]{0:T(1024)S(1)} %multiply_subtract_fusion.1, ...), kind=kOutput, calls=%fused_computation.8 | convolution fusion | flops 811597824 | bytes 9538560 | tf_op jit(solution)/shard_map/dot_general | solution.py:67
  344.0 5.8 %cholesky.96 = f32[64,64]{1,0:T(8,128)S(1)} custom-call(f32[64,64]{1,0:T(8,128)S(1)} %fusion.24), custom_call_target="Cholesky" | custom-call | tf_op jit(solution)/shard_map/jit(cholesky)/cholesky | solution.py:11
  351.2 4.9 custom-call.23
  356.1 119.0 %all-reduce.7.cloned.1.call-done = f32[64,4096]{1,0:T(8,128)} async-done(((f32[64,4096]{1,0:T(8,128)}), f32[64,4096]{1,0:T(8,128)}) %all-reduce.7.cloned.1.call-update) | async-done | bytes 1048592 | tf_op jit(solution)/shard_map/psum | solution.py:68
  475.1 2.4 fusion.20
  477.5 1.0 fusion.22
  479.5 6.6 %fusion.1 = f32[64,256]{1,0:T(8,128)S(1)} fusion(f32[64,4096]{1,0:T(8,128)S(1)} %fusion.22, f32[4096]{0:T(1024)S(1)} %multiply_subtract_fusion, f32[256]{0:T(256)S(1)} %multiply_subtract_fusion.2, f32[256,4096]{1,0:T(8,128)S(1)} %copy-done.2, f32[256,4096]{1,0:T(8,128)} %get-tuple-element.18, f32[4096]{0:T(1024)S(1)} %multiply_subtract_fusion.1, ...), kind=kOutput, calls=%fused_computation.7 | convolution fusion | flops 811597824 | bytes 9538560 | tf_op jit(solution)/shard_map/dot_general | solution.py:27
  486.2 5.8 %cholesky.107 = f32[64,64]{1,0:T(8,128)S(1)} custom-call(f32[64,64]{1,0:T(8,128)S(1)} %fusion.19), custom_call_target="Cholesky" | custom-call | tf_op jit(solution)/shard_map/jit(cholesky)/cholesky | solution.py:11
  493.4 4.9 custom-call.25
  (58 shorter events, 12.4 us)
Async XLA Ops:
  7.2 0.8 copy-start
  7.2 58.7 %all-gather.2.cloned.1.call-start = ((), (), s32[]{:S(2)}) async-start(), calls=%async_computation | async-start | bytes 1081344 | tf_op jit(solution)/shard_map/all_gather | solution.py:53
  7.9 253.7 %all-reduce.5.cloned.1.call-start = ((), (), s32[]{:S(2)}) async-start(), calls=%async_computation.1 | async-start | bytes 4194304 | tf_op jit(solution)/shard_map/psum | solution.py:68
  8.2 107.4 %copy-start.3 = (f32[4096]{0:T(1024)S(1)}, f32[4096]{0:T(1024)}, u32[]{:S(2)}) copy-start(f32[4096]{0:T(1024)} %param.20) | copy-start | bytes 49156
  8.2 107.4 %copy-start.5 = (s32[256]{0:T(256)S(1)}, s32[256]{0:T(256)}, u32[]{:S(2)}) copy-start(s32[256]{0:T(256)} %param.16) | copy-start | bytes 3076
  8.2 107.4 %copy-start.6 = (f32[256]{0:T(256)S(1)}, f32[256]{0:T(256)}, u32[]{:S(2)}) copy-start(f32[256]{0:T(256)} %param.19) | copy-start | bytes 3076
  127.6 347.5 %all-reduce.7.cloned.1.call-start = ((), (), s32[]{:S(2)}) async-start(), calls=%async_computation.2 | async-start | bytes 2097152 | tf_op jit(solution)/shard_map/psum | solution.py:68
  261.6 6.1 %copy-start.1 = (f32[256,4096]{1,0:T(8,128)S(1)}, f32[256,4096]{1,0:T(8,128)}, u32[]{:S(2)}) copy-start(f32[256,4096]{1,0:T(8,128)} %param.15) | copy-start | bytes 12582916
  335.8 143.6 %copy-start.4 = (f32[4096]{0:T(1024)}, f32[4096]{0:T(1024)S(1)}, u32[]{:S(2)}) copy-start(f32[4096]{0:T(1024)S(1)} %multiply_subtract_fusion) | copy-start | bytes 49156
  335.9 143.6 %copy-start.7 = (f32[256]{0:T(256)}, f32[256]{0:T(256)S(1)}, u32[]{:S(2)}) copy-start(f32[256]{0:T(256)S(1)} %multiply_subtract_fusion.2) | copy-start | bytes 3076
  475.1 4.4 copy-start.2
Sparse Core Ops, SparseCore 0:
  10.9 55.0 all-gather.1
  127.7 133.8 all-reduce.4
  344.1 130.8 all-reduce.6
where the time goes:
time: 515 us; the launch traced here: 507 us
  waiting for transfers between devices  289 us (56%)
  blocking collectives  80 us (16%)
  matrix products  61.4 us (12%)
  other arithmetic  49.6 us (10%)
  between operations  15.8 us (3%)
  starting transfers between devices  10.2 us (2%)
    psum x2, waiting for transfers between devices, body(): summed = lax.psum(payload, ('gx', 'gy', 'gz'))  231 us
    psum x2, blocking collectives, body(): day_sums = lax.psum(day_part, ('gx', 'gy', 'gz'))  80 us
    all_gather x1, waiting for transfers between devices, body(): lax.all_gather(factor_init, ('gx', 'gy', 'gz'), axis=1, tiled=True)  57.7 us
    another operation x12, other arithmetic, solve_spd(): lower = jnp.linalg.cholesky(matrix)  26.1 us
    another operation x8, other arithmetic, solve_spd(): lax.linalg.triangular_solve(lower, middle, left_side=True, lower=True, tr...  22.2 us
    dot_general x2, matrix products, body(): payload = jnp.dot(loading, resid, precision=lax.Precision.HIGHEST)  20 us
    dot_general x2, matrix products, contract_first(): lax.dot_general(left, right, (((0,), (0,)), ((), ())), precision=lax.Prec...  15.6 us
    dot_general x4, matrix products, contract_last(): lax.dot_general(left, right, (((1,), (1,)), ((), ())), precision=lax.Prec...  13.7 us
  transfers between devices with their start and end apart: 3, of which 3 were waited for; matrix products, arithmetic and copies ran while one was open for 5% of the time, Pallas kernels for 0%

commit v1 on v0

--- a/solution.py
+++ b/solution.py
@@ -59,7 +59,7 @@
         day_part = jnp.sum(without, 0)
         row_sums = jnp.sum(without, 1)
         resid = None
-        day_sums = lax.psum(day_part, ("gx", "gy", "gz"))
+        day_sums = lax.psum(lax.psum(day_part, ("gy", "gz")), "gx")
         grand = jnp.sum(day_sums) / (all_units * total_days)
         day_eff = day_sums / all_units - grand
         unit_eff = row_sums / total_days - grand

time: 515 us -> 552 us (1.072)
  blocking collectives: 80 us -> 164 us
  waiting for transfers between devices: 289 us -> 241 us
    psum x2 -> x6, blocking collectives: 80 us -> 164 us  [the longest x4 82.6 us: body(): day_sums = lax.psum(lax.psum(day_part, ('gy', 'gz')), 'gx')]
    all_gather x1, waiting for transfers between devices: 57.7 us -> 15.5 us  [body(): lax.all_gather(factor_init, ('gx', 'gy', 'gz'), axis=1, tiled=True)]
    psum x2, waiting for transfers between devices: 231 us -> 225 us  [body(): summed = lax.psum(payload, ('gx', 'gy', 'gz'))]
where the time goes in v1:
time: 552 us; the launch traced here: 543 us
  waiting for transfers between devices  241 us (44%)
  blocking collectives  164 us (30%)
  matrix products  61.4 us (11%)
  other arithmetic  49.6 us (9%)
  between operations  15.8 us (3%)
  starting transfers between devices  10.5 us (2%)
    psum x2, waiting for transfers between devices, body(): summed = lax.psum(payload, ('gx', 'gy', 'gz'))  225 us
    psum x4, blocking collectives, body(): day_sums = lax.psum(lax.psum(day_part, ('gy', 'gz')), 'gx')  82.6 us
    psum x2, blocking collectives, body(): unit_gram = lax.psum(contract_last(loading, loading), ('gx', 'gy', 'gz'))  81.1 us
    another operation x12, other arithmetic, solve_spd(): lower = jnp.linalg.cholesky(matrix)  26.1 us
    another operation x8, other arithmetic, solve_spd(): lax.linalg.triangular_solve(lower, middle, left_side=True, lower=True, tr...  22.2 us
    dot_general x2, matrix products, body(): payload = jnp.dot(loading, resid, precision=lax.Precision.HIGHEST)  20 us
    dot_general x2, matrix products, contract_first(): lax.dot_general(left, right, (((0,), (0,)), ((), ())), precision=lax.Prec...  15.6 us
    all_gather x1, waiting for transfers between devices, body(): lax.all_gather(factor_init, ('gx', 'gy', 'gz'), axis=1, tiled=True)  15.5 us
  transfers between devices with their start and end apart: 3, of which 3 were waited for; matrix products, arithmetic and copies ran while one was open for 5% of the time, Pallas kernels for 0%

profile of v1, /device:TPU:0, one launch (start us, length us, event | category | flops | bytes accessed | tf_op | source)
XLA Modules:
  0.0 543.1 jit_solution(18379160564300455933)
XLA Ops:
  8.2 42.1 %psum.56 = f32[64,64]{0,1:T(8,128)S(1)} all-reduce(f32[64,64]{0,1:T(8,128)S(1)} %fusion.41), channel_id=1, replica_groups=mesh['gx'=4,'gy'=4,'gz'=2] {'gx','gy','gz'}, use_global_device_ids=true, to_apply=%region_0.0 | all-reduce | flops 4096 | bytes 32768 | tf_op jit(solution)/shard_map/psum | solution.py:50
  50.5 15.5 %all-gather.2.cloned.1.call-done = f32[64,4096]{1,0:T(8,128)} async-done(((f32[64,128]{1,0:T(8,128)}), f32[64,4096]{1,0:T(8,128)}) %all-gather.2.cloned.1.call-update) | async-done | bytes 1048592 | tf_op jit(solution)/shard_map/all_gather | solution.py:53
  66.0 7.9 %subtract_reduce_fusion.3 = (f32[256]{0:T(256)S(1)}, f32[4096]{0:T(1024)S(1)}, f32[256,4096]{1,0:T(8,128)}) fusion(f32[256,4096]{1,0:T(8,128)} %param.15, f32[4096]{0:T(1024)} %param.20, f32[256]{0:T(256)} %param.19, s32[256]{0:T(256)} %param.16, f32[64,256]{1,0:T(8,128)S(1)} %copy-done, f32[64,4096]{1,0:T(8,128)} %all-gather.2.cloned.1.call-done), kind=kOutput, calls=%fused_computation.20 | convolution fusion | flops 812642048 | bytes 9538560 | tf_op jit(solution)/shard_map/dot_general | solution.py:17
  73.9 24.4 %psum.57 = f32[4096]{0:T(1024)S(1)} all-reduce(f32[4096]{0:T(1024)S(1)} %get-tuple-element.12), channel_id=1, replica_groups=mesh['gx'=4,'gy'=4,'gz'=2] {'gy','gz'}, use_global_device_ids=true, to_apply=%region_5.0 | all-reduce | flops 4096 | bytes 32768 | tf_op jit(solution)/shard_map/psum | solution.py:62
  98.4 17.4 %psum.58 = f32[4096]{0:T(1024)S(1)} all-reduce(f32[4096]{0:T(1024)S(1)} %psum.57), channel_id=1, replica_groups=mesh['gx'=4,'gy'=4,'gz'=2] {'gx'}, use_global_device_ids=true, to_apply=%region_6.0 | all-reduce | flops 4096 | bytes 32768 | tf_op jit(solution)/shard_map/psum | solution.py:62
  117.1 12.0 %convolution_bitcast_fusion = f32[64,4096]{0,1:T(8,128)} fusion(f32[64,256]{1,0:T(8,128)S(1)} %copy-done, f32[4096]{0:T(1024)S(1)} %multiply_subtract_fusion.1, f32[256]{0:T(256)S(1)} %multiply_subtract_fusion.3, f32[256,4096]{1,0:T(8,128)} %param.15, f32[256,4096]{1,0:T(8,128)} %get-tuple-element.13, f32[4096]{0:T(1024)S(1)} %copy-done.3, ...), kind=kOutput, calls=%fused_computation | convolution fusion | flops 811597824 | bytes 9538560 | tf_op jit(solution)/shard_map/dot_general | solution.py:67
  129.1 10.4 %all-reduce.5.cloned.1.call-start = ((), (), s32[]{:S(2)}) async-start(), calls=%async_computation.2 | async-start | bytes 2097152 | tf_op jit(solution)/shard_map/psum | solution.py:68
  139.5 5.8 %cholesky.74 = f32[64,64]{1,0:T(8,128)S(1)} custom-call(f32[64,64]{1,0:T(8,128)S(1)} %fusion.34), custom_call_target="Cholesky" | custom-call | tf_op jit(solution)/shard_map/jit(cholesky)/cholesky | solution.py:11
  146.7 4.9 custom-call.19
  151.6 108.8 %all-reduce.3.cloned.1.call-done = f32[64,4096]{0,1:T(8,128)} async-done(((f32[64,4096]{0,1:T(8,128)}), f32[64,4096]{0,1:T(8,128)}) %all-reduce.3.cloned.1.call-update) | async-done | bytes 1048592 | tf_op jit(solution)/shard_map/psum | solution.py:68
  266.4 6.6 %fusion = f32[64,256]{1,0:T(8,128)S(1)} fusion(f32[64,4096]{1,0:T(8,128)S(1)} %fusion.32, f32[4096]{0:T(1024)S(1)} %multiply_subtract_fusion.1, f32[256]{0:T(256)S(1)} %multiply_subtract_fusion.3, f32[256,4096]{1,0:T(8,128)S(1)} %copy-done.1, f32[256,4096]{1,0:T(8,128)} %get-tuple-element.13, f32[4096]{0:T(1024)S(1)} %copy-done.3, f32[256]{0:T(256)S(1)} %copy-done.6, ...), kind=kOutput, calls=%fused_computation.6 | convolution fusion | flops 811597824 | bytes 9538560 | tf_op jit(solution)/shard_map/dot_general | solution.py:27
  273.2 5.8 %cholesky.85 = f32[64,64]{1,0:T(8,128)S(1)} custom-call(f32[64,64]{1,0:T(8,128)S(1)} %fusion.29), custom_call_target="Cholesky" | custom-call | tf_op jit(solution)/shard_map/jit(cholesky)/cholesky | solution.py:11
  280.4 4.9 custom-call.21
  286.0 7.7 %subtract_reduce_fusion.1 = (f32[256]{0:T(256)S(1)}, f32[4096]{0:T(1024)S(1)}, f32[256,4096]{1,0:T(8,128)}) fusion(f32[256,4096]{1,0:T(8,128)} %param.15, f32[4096]{0:T(1024)S(1)} %multiply_subtract_fusion.1, f32[256]{0:T(256)S(1)} %multiply_subtract_fusion.3, s32[256]{0:T(256)S(1)} %copy-done.5, f32[64,256]{1,0:T(8,128)S(1)} %fusion.27, ...), kind=kOutput, calls=%fused_computation.18 | convolution fusion | flops 812642048 | bytes 9538560 | tf_op jit(solution)/shard_map/dot_general | solution.py:17
  293.7 39.0 %psum.60 = f32[64,64]{0,1:T(8,128)S(1)} all-reduce(f32[64,64]{0,1:T(8,128)S(1)} %fusion.42), channel_id=1, replica_groups=mesh['gx'=4,'gy'=4,'gz'=2] {'gx','gy','gz'}, use_global_device_ids=true, to_apply=%region_9.15 | all-reduce | flops 4096 | bytes 32768 | tf_op jit(solution)/shard_map/psum | solution.py:50
  332.8 23.1 %psum.61 = f32[4096]{0:T(1024)S(1)} all-reduce(f32[4096]{0:T(1024)S(1)} %get-tuple-element.10), channel_id=1, replica_groups=mesh['gx'=4,'gy'=4,'gz'=2] {'gy','gz'}, use_global_device_ids=true, to_apply=%region_12.18 | all-reduce | flops 4096 | bytes 32768 | tf_op jit(solution)/shard_map/psum | solution.py:62
  355.9 17.6 %psum.62 = f32[4096]{0:T(1024)S(1)} all-reduce(f32[4096]{0:T(1024)S(1)} %psum.61), channel_id=1, replica_groups=mesh['gx'=4,'gy'=4,'gz'=2] {'gx'}, use_global_device_ids=true, to_apply=%region_13.19 | all-reduce | flops 4096 | bytes 32768 | tf_op jit(solution)/shard_map/psum | solution.py:62
  374.8 8.1 %fusion.2 = f32[64,4096]{1,0:T(8,128)} fusion(f32[64,256]{1,0:T(8,128)S(1)} %fusion.27, f32[4096]{0:T(1024)S(1)} %multiply_subtract_fusion, f32[256]{0:T(256)S(1)} %multiply_subtract_fusion.2, f32[256,4096]{1,0:T(8,128)} %param.15, f32[256,4096]{1,0:T(8,128)} %get-tuple-element.14, f32[4096]{0:T(1024)S(1)} %multiply_subtract_fusion.1, ...), kind=kOutput, calls=%fused_computation.8 | convolution fusion | flops 811597824 | bytes 9538560 | tf_op jit(solution)/shard_map/dot_general | solution.py:67
  382.9 5.8 %cholesky.96 = f32[64,64]{1,0:T(8,128)S(1)} custom-call(f32[64,64]{1,0:T(8,128)S(1)} %fusion.24), custom_call_target="Cholesky" | custom-call | tf_op jit(solution)/shard_map/jit(cholesky)/cholesky | solution.py:11
  390.1 4.9 custom-call.23
  395.0 116.2 %all-reduce.5.cloned.1.call-done = f32[64,4096]{1,0:T(8,128)} async-done(((f32[64,4096]{1,0:T(8,128)}), f32[64,4096]{1,0:T(8,128)}) %all-reduce.5.cloned.1.call-update) | async-done | bytes 1048592 | tf_op jit(solution)/shard_map/psum | solution.py:68
  515.7 6.6 %fusion.1 = f32[64,256]{1,0:T(8,128)S(1)} fusion(f32[64,4096]{1,0:T(8,128)S(1)} %fusion.22, f32[4096]{0:T(1024)S(1)} %multiply_subtract_fusion, f32[256]{0:T(256)S(1)} %multiply_subtract_fusion.2, f32[256,4096]{1,0:T(8,128)S(1)} %copy-done.2, f32[256,4096]{1,0:T(8,128)} %get-tuple-element.14, f32[4096]{0:T(1024)S(1)} %multiply_subtract_fusion.1, ...), kind=kOutput, calls=%fused_computation.7 | convolution fusion | flops 811597824 | bytes 9538560 | tf_op jit(solution)/shard_map/dot_general | solution.py:27
  522.4 5.8 %cholesky.107 = f32[64,64]{1,0:T(8,128)S(1)} custom-call(f32[64,64]{1,0:T(8,128)S(1)} %fusion.19), custom_call_target="Cholesky" | custom-call | tf_op jit(solution)/shard_map/jit(cholesky)/cholesky | solution.py:11
  529.6 4.9 custom-call.25
  (62 shorter events, 20.8 us)
Async XLA Ops:
  7.2 0.8 copy-start
  7.2 58.8 %all-gather.2.cloned.1.call-start = ((), (), s32[]{:S(2)}) async-start(), calls=%async_computation | async-start | bytes 1081344 | tf_op jit(solution)/shard_map/all_gather | solution.py:53
  7.9 252.4 %all-reduce.3.cloned.1.call-start = ((), (), s32[]{:S(2)}) async-start(), calls=%async_computation.1 | async-start | bytes 4194304 | tf_op jit(solution)/shard_map/psum | solution.py:68
  50.5 66.6 %copy-start.3 = (f32[4096]{0:T(1024)S(1)}, f32[4096]{0:T(1024)}, u32[]{:S(2)}) copy-start(f32[4096]{0:T(1024)} %param.20) | copy-start | bytes 49156
  50.5 66.6 %copy-start.5 = (s32[256]{0:T(256)S(1)}, s32[256]{0:T(256)}, u32[]{:S(2)}) copy-start(s32[256]{0:T(256)} %param.16) | copy-start | bytes 3076
  50.5 66.6 %copy-start.6 = (f32[256]{0:T(256)S(1)}, f32[256]{0:T(256)}, u32[]{:S(2)}) copy-start(f32[256]{0:T(256)} %param.19) | copy-start | bytes 3076
  129.1 382.1 %all-reduce.5.cloned.1.call-start = ((), (), s32[]{:S(2)}) async-start(), calls=%async_computation.2 | async-start | bytes 2097152 | tf_op jit(solution)/shard_map/psum | solution.py:68
  260.4 6.1 %copy-start.1 = (f32[256,4096]{1,0:T(8,128)S(1)}, f32[256,4096]{1,0:T(8,128)}, u32[]{:S(2)}) copy-start(f32[256,4096]{1,0:T(8,128)} %param.15) | copy-start | bytes 12582916
  374.8 140.9 %copy-start.4 = (f32[4096]{0:T(1024)}, f32[4096]{0:T(1024)S(1)}, u32[]{:S(2)}) copy-start(f32[4096]{0:T(1024)S(1)} %multiply_subtract_fusion) | copy-start | bytes 49156
  374.8 140.9 %copy-start.7 = (f32[256]{0:T(256)}, f32[256]{0:T(256)S(1)}, u32[]{:S(2)}) copy-start(f32[256]{0:T(256)S(1)} %multiply_subtract_fusion.2) | copy-start | bytes 3076
  511.2 4.5 copy-start.2
Sparse Core Ops, SparseCore 0:
  10.9 55.1 all-gather.1
  129.2 131.0 all-reduce.2
  383.0 128.1 all-reduce.4
